TPU v7x, 32 devices: a whole 2x2x4 slice. The times are simulated.
32 devices in a mesh: seq: 16 (over z, x, core), grp: 2 (over y).
Axes of the slice: x: 2, y: 2, z: 4, core: 2. Of those that a mesh axis runs over, the one named last changes fastest.
Arguments:
- out_grad: bfloat16 [2, 3456, 1024], P('grp', 'seq'), may hold values from -6 to 6
- combine_logits: float32 [2, 3456, 64], P('grp', 'seq'), may hold values from -20 to 330
- expert_out: bfloat16 [2, 64, 1024], P('grp', 'seq'), may hold values from -6 to 6
- slot_in: bfloat16 [2, 64, 1024], P('grp', 'seq'), may hold values from -6 to 6
- router: bfloat16 [64, 1024], P('seq'), may hold values from -0.1875 to 0.1875
- w_gate: bfloat16 [64, 2048, 1024], P('seq', 'grp'), may hold values from -0.1875 to 0.1875
- w_up: bfloat16 [64, 2048, 1024], P('seq', 'grp'), may hold values from -0.1875 to 0.1875
- w_down: bfloat16 [64, 2048, 1024], P('seq', 'grp'), may hold values from -0.125 to 0.125
Outputs:
- token_grad: bfloat16 [2, 3456, 1024], P('grp', 'seq')
- slot_grad: float32 [2, 64, 1024], P('grp', 'seq')
- grad_gate: bfloat16 [64, 2048, 1024], P('seq', 'grp')
- grad_up: bfloat16 [64, 2048, 1024], P('seq', 'grp')
- grad_down: bfloat16 [64, 2048, 1024], P('seq', 'grp')
All inputs are finite; a program needn't handle non-finite values.
Results may differ from a plain program's by a relative error of at most 0.028.
Values may be sent and summed in bfloat16 or wider, within the bound.
A program may use at most 128 MiB of HBM per device.

v0:
```python
import functools

import jax
import jax.numpy as jnp
from jax import lax
from jax.experimental import pallas as pl
from jax.experimental.pallas import tpu as pltpu
from jax.sharding import PartitionSpec as P

MESH = pl.DeviceIdType.MESH
F32 = jnp.float32
BF16 = jnp.bfloat16
NT = (((1,), (1,)), ((), ()))
TN = (((0,), (0,)), ((), ()))


def rows_of(ref, count):
    return jnp.concatenate([ref[i].astype(F32) for i in range(count)], axis=0).astype(BF16)


def exchange_kernel(
    nseq, ngrp,
    grad_hbm, logit_hbm, eout_hbm, slot_hbm, router_hbm, gate_hbm, up_hbm, down_hbm,
    acts_ref, pair_ref, lgrad_ref, rout_ref, sgrad_ref,
    grad, logit, gate_w, up_w, down_w, part_out, part_in, pieces, slots, outs, back_out, back_in,
    load_sem, w_sem, part_ssem, part_rsem, piece_ssem, piece_rsem,
    slot_ssem, slot_rsem, out_ssem, out_rsem, back_ssem, back_rsem,
):
    s_me = lax.axis_index("seq")
    g_me = lax.axis_index("grp")
    experts = slots.shape[1]

    barrier = pltpu.get_barrier_semaphore()

    def greet_seq(d, c):
        pl.semaphore_signal(barrier, inc=1, device_id={"seq": lax.rem(s_me + d, nseq)}, device_id_type=MESH)
        return c

    def greet_grp(d, c):
        pl.semaphore_signal(barrier, inc=1, device_id={"grp": lax.rem(g_me + d, ngrp)}, device_id_type=MESH)
        return c

    lax.fori_loop(1, ngrp, greet_grp, 0)
    lax.fori_loop(1, nseq, greet_seq, 0)

    loads = [
        pltpu.make_async_copy(logit_hbm, logit, load_sem.at[0]),
        pltpu.make_async_copy(grad_hbm.at[0], grad, load_sem.at[1]),
        pltpu.make_async_copy(slot_hbm.at[0], slots.at[g_me], load_sem.at[2]),
        pltpu.make_async_copy(eout_hbm.at[0], pieces.at[s_me, 0], load_sem.at[3]),
        pltpu.make_async_copy(router_hbm, pieces.at[s_me, 1], load_sem.at[4]),
    ]
    for c in loads:
        c.start()
    w_loads = {}
    for m, (src, dst) in enumerate(((gate_hbm, gate_w), (up_hbm, up_w), (down_hbm, down_w))):
        for e in range(experts):
            w_loads[m, e] = pltpu.make_async_copy(src.at[e], dst.at[e], w_sem.at[m, e])
    for e in range(experts):
        w_loads[0, e].start()
        w_loads[1, e].start()
    for e in range(experts):
        w_loads[2, e].start()

    def part_copy(d):
        to = lax.rem(s_me + d, nseq)
        return pltpu.make_async_remote_copy(
            src_ref=part_out.at[to], dst_ref=part_in.at[s_me],
            send_sem=part_ssem.at[to], recv_sem=part_rsem.at[s_me],
            device_id={"seq": to}, device_id_type=MESH)

    def piece_copy(d):
        to = lax.rem(s_me + d, nseq)
        return pltpu.make_async_remote_copy(
            src_ref=pieces.at[s_me], dst_ref=pieces.at[s_me],
            send_sem=piece_ssem.at[to], recv_sem=piece_rsem.at[s_me],
            device_id={"seq": to}, device_id_type=MESH)

    def grp_copy(d, src, dst, ssem, rsem):
        to = lax.rem(g_me + d, ngrp)
        return pltpu.make_async_remote_copy(
            src_ref=src.at[to] if src is not dst else src.at[g_me], dst_ref=dst.at[g_me],
            send_sem=ssem.at[to], recv_sem=rsem.at[g_me],
            device_id={"grp": to}, device_id_type=MESH)

    def seq_arrived(d, buf, rsem, ssem):
        at = lax.rem(s_me + d, nseq)
        pltpu.make_async_remote_copy(
            src_ref=buf.at[at], dst_ref=buf.at[at], send_sem=ssem.at[at], recv_sem=rsem.at[at],
            device_id={"seq": at}, device_id_type=MESH).wait_recv()

    def grp_arrived(d, buf, rsem, ssem):
        at = lax.rem(g_me + d, ngrp)
        pltpu.make_async_remote_copy(
            src_ref=buf.at[at], dst_ref=buf.at[at], send_sem=ssem.at[at], recv_sem=rsem.at[at],
            device_id={"grp": at}, device_id_type=MESH).wait_recv()

    def each(low, high, fn):
        def step(d, c):
            fn(d)
            return c
        lax.fori_loop(low, high, step, 0)

    loads[0].wait()
    z = logit[...]
    z = jnp.exp(z - jnp.max(z, axis=0, keepdims=True))
    probs = z / jnp.sum(z, axis=0, keepdims=True)
    logit[...] = probs
    loads[1].wait()
    share = jnp.dot(probs.astype(BF16), grad[...], preferred_element_type=F32)
    for j in range(nseq):
        part_out[j] = share[j * experts:(j + 1) * experts].astype(BF16)
    part_in[s_me] = part_out[s_me]
    for c in loads[2:]:
        c.wait()

    pl.semaphore_wait(barrier, (nseq - 1) + (ngrp - 1))
    each(1, ngrp, lambda d: grp_copy(d, slots, slots, slot_ssem, slot_rsem).start())
    each(1, nseq, lambda d: part_copy(d).start())
    each(1, nseq, lambda d: piece_copy(d).start())

    rows = ngrp * experts
    width = gate_w.shape[1]
    own = lax.rem(lax.broadcasted_iota(jnp.int32, (rows, width), 0), experts)

    each(1, ngrp, lambda d: grp_arrived(d, slots, slot_rsem, slot_ssem))
    x = rows_of(slots, ngrp)
    pair_ref[0] = x

    gate = jnp.zeros((rows, width), F32)
    upper = jnp.zeros((rows, width), F32)

    def project(e, gate, upper):
        w_loads[0, e].wait()
        gate = jnp.where(own == e, lax.dot_general(x, gate_w[e], NT, preferred_element_type=F32), gate)
        w_loads[1, e].wait()
        upper = jnp.where(own == e, lax.dot_general(x, up_w[e], NT, preferred_element_type=F32), upper)
        return gate, upper

    early = experts // 2
    for e in range(early):
        gate, upper = project(e, gate, upper)

    each(1, nseq, lambda d: seq_arrived(d, part_in, part_rsem, part_ssem))
    outs[g_me] = jnp.sum(part_in[...].astype(F32), axis=0).astype(BF16)
    each(1, ngrp, lambda d: grp_copy(d, outs, outs, out_ssem, out_rsem).start())

    for e in range(early, experts):
        gate, upper = project(e, gate, upper)
    sig = jax.nn.sigmoid(gate)
    act = gate * sig
    acts_ref[2] = (act * upper).astype(BF16)

    each(1, ngrp, lambda d: grp_arrived(d, outs, out_rsem, out_ssem))
    so = rows_of(outs, ngrp)
    pair_ref[1] = so
    hgrad = jnp.zeros((rows, width), F32)
    for e in range(experts):
        w_loads[2, e].wait()
        hgrad = jnp.where(own == e, lax.dot_general(so, down_w[e], NT, preferred_element_type=F32), hgrad)
    up_grad = (hgrad * gate * sig).astype(BF16)
    gate_grad = (hgrad * upper * sig * (1.0 + gate * (1.0 - sig))).astype(BF16)
    acts_ref[0] = gate_grad
    acts_ref[1] = up_grad

    gate_f, up_f = gate_grad.astype(F32), up_grad.astype(F32)
    total = jnp.zeros((rows, x.shape[1]), F32)
    for e in range(experts):
        total += jnp.dot(jnp.where(own == e, gate_f, 0.0).astype(BF16), gate_w[e], preferred_element_type=F32)
        total += jnp.dot(jnp.where(own == e, up_f, 0.0).astype(BF16), up_w[e], preferred_element_type=F32)
    for g in range(ngrp):
        back_out[g] = total[g * experts:(g + 1) * experts].astype(BF16)
    back_in[g_me] = back_out[g_me]
    each(1, ngrp, lambda d: grp_copy(d, back_out, back_in, back_ssem, back_rsem).start())

    each(1, nseq, lambda d: seq_arrived(d, pieces, piece_rsem, piece_ssem))
    eout = rows_of(pieces.at[:, 0], nseq)
    rout_ref[...] = rows_of(pieces.at[:, 1], nseq)
    wgrad = lax.dot_general(eout, grad[...], NT, preferred_element_type=F32)
    p = logit[...]
    centre = jnp.sum(wgrad * p, axis=0, keepdims=True)
    lgrad_ref[...] = (p * (wgrad - centre)).astype(BF16)

    each(1, ngrp, lambda d: grp_arrived(d, back_in, back_rsem, back_ssem))
    sgrad_ref[...] = jnp.sum(back_in[...].astype(F32), axis=0)

    each(1, nseq, lambda d: part_copy(d).wait_send())
    each(1, nseq, lambda d: piece_copy(d).wait_send())
    each(1, ngrp, lambda d: grp_copy(d, slots, slots, slot_ssem, slot_rsem).wait_send())
    each(1, ngrp, lambda d: grp_copy(d, outs, outs, out_ssem, out_rsem).wait_send())
    each(1, ngrp, lambda d: grp_copy(d, back_out, back_in, back_ssem, back_rsem).wait_send())


def write_kernel(
    experts, cut,
    acts_ref, pair_ref, lgrad_ref, rout_ref, sgrad_in,
    tgrad_hbm, sgrad_hbm, gg_hbm, gu_hbm, gd_hbm,
    staged, tokens, sem, small_sem,
):
    outs = (gg_hbm, gu_hbm, gd_hbm)
    width = acts_ref.shape[2]
    own = lax.rem(lax.broadcasted_iota(jnp.int32, acts_ref.shape[1:], 0), experts)

    def chunk(k, e, j):
        at = pl.ds(j * cut, cut)
        return pltpu.make_async_copy(staged.at[k, e, at], outs[k].at[e, at], sem.at[k, e, j])

    def expert(e, c):
        for k, src in enumerate((0, 0, 1)):
            a = jnp.where(own == e, acts_ref[k].astype(F32), 0.0).astype(BF16)
            for j in range(width // cut):
                at = slice(j * cut, (j + 1) * cut)
                staged[k, e, at] = lax.dot_general(
                    a[:, at], pair_ref[src], TN, preferred_element_type=F32).astype(BF16)
                chunk(k, e, j).start()
        return c

    lax.fori_loop(0, experts, expert, 0)
    tokens[...] = lax.dot_general(lgrad_ref[...], rout_ref[...], TN, preferred_element_type=F32).astype(BF16)
    small = [
        pltpu.make_async_copy(tokens, tgrad_hbm.at[0], small_sem.at[0]),
        pltpu.make_async_copy(sgrad_in, sgrad_hbm.at[0], small_sem.at[1]),
    ]
    for c in small:
        c.start()
    for e in range(experts):
        for k in range(3):
            for j in range(width // cut):
                chunk(k, e, j).wait()
    for c in small:
        c.wait()


def per_device(nseq, ngrp, out_grad, combine_logits, expert_out, slot_in, router, w_gate, w_up, w_down):
    _, tokens, dim = out_grad.shape
    total_experts = combine_logits.shape[2]
    experts, width, _ = w_gate.shape
    rows = ngrp * experts
    DMA = pltpu.SemaphoreType.DMA
    anyspec = pl.BlockSpec(memory_space=pltpu.HBM)
    vspec = pl.BlockSpec(memory_space=pltpu.VMEM)
    acts, pair, lgrad, rout, sgrad = pl.pallas_call(
        functools.partial(exchange_kernel, nseq, ngrp),
        out_shape=(
            jax.ShapeDtypeStruct((3, rows, width), BF16),
            jax.ShapeDtypeStruct((2, rows, dim), BF16),
            jax.ShapeDtypeStruct((total_experts, tokens), BF16),
            jax.ShapeDtypeStruct((total_experts, dim), BF16),
            jax.ShapeDtypeStruct((experts, dim), F32),
        ),
        in_specs=[anyspec] * 8,
        out_specs=(vspec,) * 5,
        scratch_shapes=[
            pltpu.VMEM((tokens, dim), BF16),
            pltpu.VMEM((total_experts, tokens), F32),
            pltpu.VMEM((experts, width, dim), BF16),
            pltpu.VMEM((experts, width, dim), BF16),
            pltpu.VMEM((experts, width, dim), BF16),
            pltpu.VMEM((nseq, experts, dim), BF16),
            pltpu.VMEM((nseq, experts, dim), BF16),
            pltpu.VMEM((nseq, 2, experts, dim), BF16),
            pltpu.VMEM((ngrp, experts, dim), BF16),
            pltpu.VMEM((ngrp, experts, dim), BF16),
            pltpu.VMEM((ngrp, experts, dim), BF16),
            pltpu.VMEM((ngrp, experts, dim), BF16),
            DMA((5,)), DMA((3, experts)),
            DMA((nseq,)), DMA((nseq,)), DMA((nseq,)), DMA((nseq,)),
            DMA((ngrp,)), DMA((ngrp,)), DMA((ngrp,)), DMA((ngrp,)), DMA((ngrp,)), DMA((ngrp,)),
        ],
        compiler_params=pltpu.CompilerParams(
            collective_id=0, has_side_effects=True, vmem_limit_bytes=48 * 1024 * 1024),
        name="exchange",
    )(*(pltpu.with_memory_space_constraint(a, pltpu.HBM) for a in (
        out_grad, jnp.transpose(combine_logits[0]), expert_out, slot_in, router, w_gate, w_up, w_down)))

    cut = 256 if width % 256 == 0 else width
    return pl.pallas_call(
        functools.partial(write_kernel, experts, cut),
        out_shape=(
            jax.ShapeDtypeStruct((1, tokens, dim), BF16),
            jax.ShapeDtypeStruct((1, experts, dim), F32),
        ) + (jax.ShapeDtypeStruct((experts, width, dim), BF16),) * 3,
        in_specs=[vspec] * 5,
        out_specs=(pl.BlockSpec(memory_space=pltpu.HBM),) * 5,
        scratch_shapes=[
            pltpu.VMEM((3, experts, width, dim), BF16),
            pltpu.VMEM((tokens, dim), BF16),
            DMA((3, experts, width // cut)),
            DMA((2,)),
        ],
        compiler_params=pltpu.CompilerParams(vmem_limit_bytes=40 * 1024 * 1024),
        name="write",
    )(acts, pair, lgrad, rout, sgrad)


def solution(mesh):
    return jax.shard_map(
        functools.partial(per_device, mesh.shape["seq"], mesh.shape["grp"]),
        mesh=mesh,
        in_specs=(
            P("grp", "seq", None),
            P("grp", "seq", None),
            P("grp", "seq", None),
            P("grp", "seq", None),
            P("seq", None),
            P("seq", "grp", None),
            P("seq", "grp", None),
            P("seq", "grp", None),
        ),
        out_specs=(
            P("grp", "seq", None),
            P("grp", "seq", None),
            P("seq", "grp", None),
            P("seq", "grp", None),
            P("seq", "grp", None),
        ),
        check_vma=False,
    )
```

profile of v0, /device:TPU:0, one launch (start us, length us, event | category | flops | bytes accessed | tf_op | source)
XLA Modules:
  0.0 37.1 jit_solution(5124203022002705368)
XLA Ops:
  0.6 27.3 %exchange.1 = (bf16[3,8,1024]{2,1,0:T(8,128)(2,1)S(1)}, bf16[2,8,1024]{2,1,0:T(8,128)(2,1)S(1)}, bf16[64,216]{1,0:T(8,128)(2,1)S(1)}, bf16[64,1024]{1,0:T(8,128)(2,1)S(1)}, f32[4,1024]{1,0:T(4,128)S(1)}) custom-call(bf16[1,216,1024]{2,1,0:T(8,128)(2,1)} %grad_hbm.1, f32[64,216]{1,0:T(8,128)} %bitcast.3, bf16[1,4,1024]{2,1,0:T(4,128)(2,1)} %eout_hbm.1, ...), custom_call_target="tpu_custom_call" | custom-call | tf_op jit(solution)/shard_map/exchange/pallas_call | solution.py:242
  27.9 9.2 %write.1 = (bf16[1,216,1024]{2,1,0:T(8,128)(2,1)}, f32[1,4,1024]{2,1,0:T(4,128)}, bf16[4,1024,1024]{2,1,0:T(8,128)(2,1)}, bf16[4,1024,1024]{2,1,0:T(8,128)(2,1)}, bf16[4,1024,1024]{2,1,0:T(8,128)(2,1)}) custom-call(bf16[3,8,1024]{2,1,0:T(8,128)(2,1)S(1)} %get-tuple-element.10.acts_ref, bf16[2,8,1024]{2,1,0:T(8,128)(2,1)S(1)} %get-tuple-element.11.pair_ref, ...), custom_call_target="tpu_custom_call" | custom-call | tf_op jit(solution)/shard_map/write/pallas_call | solution.py:277
where the time goes:
time: 37.8 us; the launch traced here: 37.1 us
  Pallas kernels  36.5 us (97%)
  between operations  0.64 us (2%)
    pallas_call x1, Pallas kernels, per_device(): pl.pallas_call(functools.partial(exchange_kernel, nseq, ngrp), out_shape=...  27.3 us
    pallas_call x1, Pallas kernels, per_device(): pl.pallas_call(functools.partial(write_kernel, experts, cut), out_shape=(...  9.2 us

commit v1 on v0

v1 whole, which is shorter than its diff:
```python
import functools

import jax
import jax.numpy as jnp
from jax import lax
from jax.experimental import pallas as pl
from jax.experimental.pallas import tpu as pltpu
from jax.sharding import PartitionSpec as P

MESH = pl.DeviceIdType.MESH
F32 = jnp.float32
BF16 = jnp.bfloat16
NT = (((1,), (1,)), ((), ()))
TN = (((0,), (0,)), ((), ()))


def rows_of(ref, count):
    return jnp.concatenate([ref[i].astype(F32) for i in range(count)], axis=0).astype(BF16)


def exchange_kernel(
    nseq, ngrp,
    grad_hbm, logit_hbm, eout_hbm, slot_hbm, router_hbm, gate_hbm, up_hbm, down_hbm,
    gate_w, up_w, down_w, grad, probs_ref, acts_ref, hid_ref, pair_ref, eout_ref, rout_ref,
    part_out, part_in, pieces, slots, outs,
    load_sem, w_sem, part_ssem, part_rsem, piece_ssem, piece_rsem,
    slot_ssem, slot_rsem, out_ssem, out_rsem,
):
    s_me = lax.axis_index("seq")
    g_me = lax.axis_index("grp")
    experts = slots.shape[1]

    barrier = pltpu.get_barrier_semaphore()

    def greet_seq(d, c):
        pl.semaphore_signal(barrier, inc=1, device_id={"seq": lax.rem(s_me + d, nseq)}, device_id_type=MESH)
        return c

    def greet_grp(d, c):
        pl.semaphore_signal(barrier, inc=1, device_id={"grp": lax.rem(g_me + d, ngrp)}, device_id_type=MESH)
        return c

    lax.fori_loop(1, ngrp, greet_grp, 0)
    lax.fori_loop(1, nseq, greet_seq, 0)

    loads = [
        pltpu.make_async_copy(logit_hbm, probs_ref, load_sem.at[0]),
        pltpu.make_async_copy(grad_hbm.at[0], grad, load_sem.at[1]),
        pltpu.make_async_copy(slot_hbm.at[0], slots.at[g_me], load_sem.at[2]),
        pltpu.make_async_copy(eout_hbm.at[0], pieces.at[s_me, 0], load_sem.at[3]),
        pltpu.make_async_copy(router_hbm, pieces.at[s_me, 1], load_sem.at[4]),
    ]
    for c in loads:
        c.start()
    w_loads = {}
    for m, (src, dst) in enumerate(((gate_hbm, gate_w), (up_hbm, up_w), (down_hbm, down_w))):
        for e in range(experts):
            w_loads[m, e] = pltpu.make_async_copy(src.at[e], dst.at[e], w_sem.at[m, e])

    def part_copy(d):
        to = lax.rem(s_me + d, nseq)
        return pltpu.make_async_remote_copy(
            src_ref=part_out.at[to], dst_ref=part_in.at[s_me],
            send_sem=part_ssem.at[to], recv_sem=part_rsem.at[s_me],
            device_id={"seq": to}, device_id_type=MESH)

    def piece_copy(d):
        to = lax.rem(s_me + d, nseq)
        return pltpu.make_async_remote_copy(
            src_ref=pieces.at[s_me], dst_ref=pieces.at[s_me],
            send_sem=piece_ssem.at[to], recv_sem=piece_rsem.at[s_me],
            device_id={"seq": to}, device_id_type=MESH)

    def grp_copy(d, buf, ssem, rsem):
        to = lax.rem(g_me + d, ngrp)
        return pltpu.make_async_remote_copy(
            src_ref=buf.at[g_me], dst_ref=buf.at[g_me],
            send_sem=ssem.at[to], recv_sem=rsem.at[g_me],
            device_id={"grp": to}, device_id_type=MESH)

    def seq_arrived(d, buf, rsem, ssem):
        at = lax.rem(s_me + d, nseq)
        pltpu.make_async_remote_copy(
            src_ref=buf.at[at], dst_ref=buf.at[at], send_sem=ssem.at[at], recv_sem=rsem.at[at],
            device_id={"seq": at}, device_id_type=MESH).wait_recv()

    def grp_arrived(d, buf, rsem, ssem):
        at = lax.rem(g_me + d, ngrp)
        pltpu.make_async_remote_copy(
            src_ref=buf.at[at], dst_ref=buf.at[at], send_sem=ssem.at[at], recv_sem=rsem.at[at],
            device_id={"grp": at}, device_id_type=MESH).wait_recv()

    def each(low, high, fn):
        def step(d, c):
            fn(d)
            return c
        lax.fori_loop(low, high, step, 0)

    loads[0].wait()
    z = probs_ref[...]
    z = jnp.exp(z - jnp.max(z, axis=0, keepdims=True))
    probs = z / jnp.sum(z, axis=0, keepdims=True)
    probs_ref[...] = probs
    loads[1].wait()
    for e in range(experts):
        w_loads[0, e].start()
        w_loads[1, e].start()
    for e in range(experts):
        w_loads[2, e].start()
    share = jnp.dot(probs.astype(BF16), grad[...], preferred_element_type=F32)
    for j in range(nseq):
        part_out[j] = share[j * experts:(j + 1) * experts].astype(BF16)
    part_in[s_me] = part_out[s_me]
    for c in loads[2:]:
        c.wait()

    pl.semaphore_wait(barrier, (nseq - 1) + (ngrp - 1))
    each(1, ngrp, lambda d: grp_copy(d, slots, slot_ssem, slot_rsem).start())
    each(1, nseq, lambda d: part_copy(d).start())
    each(1, nseq, lambda d: piece_copy(d).start())

    rows = ngrp * experts
    width = gate_w.shape[1]
    own = lax.rem(lax.broadcasted_iota(jnp.int32, (rows, width), 0), experts)

    each(1, ngrp, lambda d: grp_arrived(d, slots, slot_rsem, slot_ssem))
    x = rows_of(slots, ngrp)
    pair_ref[0] = x

    gate = jnp.zeros((rows, width), F32)
    upper = jnp.zeros((rows, width), F32)

    def project(e, gate, upper):
        w_loads[0, e].wait()
        gate = jnp.where(own == e, lax.dot_general(x, gate_w[e], NT, preferred_element_type=F32), gate)
        w_loads[1, e].wait()
        upper = jnp.where(own == e, lax.dot_general(x, up_w[e], NT, preferred_element_type=F32), upper)
        return gate, upper

    early = experts // 2
    for e in range(early):
        gate, upper = project(e, gate, upper)

    each(1, nseq, lambda d: seq_arrived(d, part_in, part_rsem, part_ssem))
    outs[g_me] = jnp.sum(part_in[...].astype(F32), axis=0).astype(BF16)
    each(1, ngrp, lambda d: grp_copy(d, outs, out_ssem, out_rsem).start())

    for e in range(early, experts):
        gate, upper = project(e, gate, upper)
    sig = jax.nn.sigmoid(gate)
    act = gate * sig
    hid_ref[...] = (act * upper).astype(BF16)
    acts_ref[0] = upper * sig * (1.0 + gate * (1.0 - sig))
    acts_ref[1] = act

    for e in range(experts):
        w_loads[2, e].wait()
    each(1, ngrp, lambda d: grp_arrived(d, outs, out_rsem, out_ssem))
    pair_ref[1] = rows_of(outs, ngrp)

    each(1, nseq, lambda d: seq_arrived(d, pieces, piece_rsem, piece_ssem))
    eout_ref[...] = rows_of(pieces.at[:, 0], nseq)
    rout_ref[...] = rows_of(pieces.at[:, 1], nseq)

    each(1, nseq, lambda d: part_copy(d).wait_send())
    each(1, nseq, lambda d: piece_copy(d).wait_send())
    each(1, ngrp, lambda d: grp_copy(d, slots, slot_ssem, slot_rsem).wait_send())
    each(1, ngrp, lambda d: grp_copy(d, outs, out_ssem, out_rsem).wait_send())


def mxu_outer(a, v, cut, store):
    for j in range(a.shape[1] // cut):
        at = slice(j * cut, (j + 1) * cut)
        store(j, lax.dot_general(a[:, at], v, TN, preferred_element_type=F32).astype(BF16))


def vpu_outer(a_cols, v_rows, cut, store):
    for j in range(a_cols[0].shape[0] // cut):
        at = slice(j * cut, (j + 1) * cut)
        total = a_cols[0][at] * v_rows[0]
        for a, v in zip(a_cols[1:], v_rows[1:]):
            total += a[at] * v
        store(j, total.astype(BF16))


def first_kernel(
    experts, cut,
    gate_w, up_w, down_w, acts_ref, hid_ref, pair_ref,
    gg_ref, mine_ref, send_ref, gu_hbm, gd_hbm,
    staged, sem,
):
    outs = (gd_hbm, gu_hbm)
    rows, width = hid_ref.shape
    ngrp = rows // experts
    own = lax.rem(lax.broadcasted_iota(jnp.int32, (rows, width), 0), experts)

    def chunk(k, e, j):
        at = pl.ds(j * cut, cut)
        return pltpu.make_async_copy(staged.at[k, e, at], outs[k].at[e, at], sem.at[k, e, j])

    def put(k, e):
        def store(j, value):
            staged[k, e, j * cut:(j + 1) * cut] = value
            chunk(k, e, j).start()
        return store

    x, so = pair_ref[0], pair_ref[1]
    hid = hid_ref[...].astype(F32)
    total = jnp.zeros((rows, x.shape[1]), F32)
    gate_all = jnp.zeros((rows, width), F32)
    for e in range(experts):
        mine = own == e
        mxu_outer(jnp.where(mine, hid, 0.0).astype(BF16), so, cut, put(0, e))
        hgrad = lax.dot_general(so, down_w[e], NT, preferred_element_type=F32)
        up_grad = jnp.where(mine, hgrad * acts_ref[1], 0.0).astype(BF16)
        gate_f = jnp.where(mine, hgrad * acts_ref[0], 0.0)
        gate_all += gate_f
        mxu_outer(up_grad, x, cut, put(1, e))
        total += jnp.dot(gate_f.astype(BF16), gate_w[e], preferred_element_type=F32)
        total += jnp.dot(up_grad, up_w[e], preferred_element_type=F32)
    gg_ref[...] = gate_all.astype(BF16)
    g_me = lax.axis_index("grp")
    for d in range(ngrp):
        at = lax.rem(g_me + d, ngrp)
        piece = jnp.zeros((experts, total.shape[1]), F32)
        for g in range(ngrp):
            piece = jnp.where(at == g, total[g * experts:(g + 1) * experts], piece)
        if d == 0:
            mine_ref[...] = piece
        else:
            send_ref[d - 1] = piece.astype(BF16)
    for k in range(2):
        for e in range(experts):
            for j in range(width // cut):
                chunk(k, e, j).wait()


def second_kernel(
    experts, cut,
    gg_ref, pair_ref, probs_ref, grad_ref, eout_ref, rout_ref,
    tgrad_hbm, gg_hbm,
    staged, tokens, sem, small_sem,
):
    rows, width = gg_ref.shape
    own = lax.rem(lax.broadcasted_iota(jnp.int32, (rows, width), 0), experts)

    def chunk(e, j):
        at = pl.ds(j * cut, cut)
        return pltpu.make_async_copy(staged.at[e, at], gg_hbm.at[e, at], sem.at[e, j])

    def put(e):
        def store(j, value):
            staged[e, j * cut:(j + 1) * cut] = value
            chunk(e, j).start()
        return store

    x = pair_ref[0]
    gate_grad = gg_ref[...].astype(F32)
    for e in range(experts):
        mxu_outer(jnp.where(own == e, gate_grad, 0.0).astype(BF16), x, cut, put(e))
        if e == 0:
            wgrad = lax.dot_general(eout_ref[...], grad_ref[...], NT, preferred_element_type=F32)
            p = probs_ref[...]
            centre = jnp.sum(wgrad * p, axis=0, keepdims=True)
            lgrad = (p * (wgrad - centre)).astype(BF16)
            tokens[...] = lax.dot_general(lgrad, rout_ref[...], TN, preferred_element_type=F32).astype(BF16)
            small = pltpu.make_async_copy(tokens, tgrad_hbm.at[0], small_sem.at[0])
            small.start()
    for e in range(experts):
        for j in range(width // cut):
            chunk(e, j).wait()
    small.wait()


def per_device(nseq, ngrp, out_grad, combine_logits, expert_out, slot_in, router, w_gate, w_up, w_down):
    _, tokens, dim = out_grad.shape
    total_experts = combine_logits.shape[2]
    experts, width, _ = w_gate.shape
    rows = ngrp * experts
    DMA = pltpu.SemaphoreType.DMA
    hspec = pl.BlockSpec(memory_space=pltpu.HBM)
    vspec = pl.BlockSpec(memory_space=pltpu.VMEM)
    weights = jax.ShapeDtypeStruct((experts, width, dim), BF16)
    gate_w, up_w, down_w, grad, probs, acts, hid, pair, eout, rout = pl.pallas_call(
        functools.partial(exchange_kernel, nseq, ngrp),
        out_shape=(
            weights, weights, weights,
            jax.ShapeDtypeStruct((tokens, dim), BF16),
            jax.ShapeDtypeStruct((total_experts, tokens), F32),
            jax.ShapeDtypeStruct((2, rows, width), F32),
            jax.ShapeDtypeStruct((rows, width), BF16),
            jax.ShapeDtypeStruct((2, rows, dim), BF16),
            jax.ShapeDtypeStruct((total_experts, dim), BF16),
            jax.ShapeDtypeStruct((total_experts, dim), BF16),
        ),
        in_specs=[hspec] * 8,
        out_specs=(vspec,) * 10,
        scratch_shapes=[
            pltpu.VMEM((nseq, experts, dim), BF16),
            pltpu.VMEM((nseq, experts, dim), BF16),
            pltpu.VMEM((nseq, 2, experts, dim), BF16),
            pltpu.VMEM((ngrp, experts, dim), BF16),
            pltpu.VMEM((ngrp, experts, dim), BF16),
            DMA((5,)), DMA((3, experts)),
            DMA((nseq,)), DMA((nseq,)), DMA((nseq,)), DMA((nseq,)),
            DMA((ngrp,)), DMA((ngrp,)), DMA((ngrp,)), DMA((ngrp,)),
        ],
        compiler_params=pltpu.CompilerParams(
            collective_id=0, has_side_effects=True, vmem_limit_bytes=8 * 1024 * 1024),
        name="exchange",
    )(*(pltpu.with_memory_space_constraint(a, pltpu.HBM) for a in (
        out_grad, jnp.transpose(combine_logits[0]), expert_out, slot_in, router, w_gate, w_up, w_down)))

    cut = 256 if width % 256 == 0 else width
    gate_grad, mine, sends, grad_up, grad_down = pl.pallas_call(
        functools.partial(first_kernel, experts, cut),
        out_shape=(
            jax.ShapeDtypeStruct((rows, width), BF16),
            jax.ShapeDtypeStruct((experts, dim), F32),
            jax.ShapeDtypeStruct((max(ngrp - 1, 1), experts, dim), BF16),
            weights, weights,
        ),
        in_specs=[vspec] * 6,
        out_specs=(vspec,) * 3 + (hspec,) * 2,
        scratch_shapes=[
            pltpu.VMEM((2, experts, width, dim), BF16),
            DMA((2, experts, width // cut)),
        ],
        compiler_params=pltpu.CompilerParams(vmem_limit_bytes=20 * 1024 * 1024),
        name="first",
    )(gate_w, up_w, down_w, acts, hid, pair)

    got = [
        lax.ppermute(sends[d - 1], "grp", [(g, (g + d) % ngrp) for g in range(ngrp)])
        for d in range(1, ngrp)
    ]

    token_grad, grad_gate = pl.pallas_call(
        functools.partial(second_kernel, experts, cut),
        out_shape=(jax.ShapeDtypeStruct((1, tokens, dim), BF16), weights),
        in_specs=[vspec] * 6,
        out_specs=(hspec,) * 2,
        scratch_shapes=[
            pltpu.VMEM((experts, width, dim), BF16),
            pltpu.VMEM((tokens, dim), BF16),
            DMA((experts, width // cut)),
            DMA((1,)),
        ],
        compiler_params=pltpu.CompilerParams(vmem_limit_bytes=12 * 1024 * 1024),
        cost_estimate=pl.CostEstimate(
            flops=0, bytes_accessed=experts * width * dim * 2, transcendentals=0),
        name="second",
    )(gate_grad, pair, probs, grad, eout, rout)
    slot_grad = mine
    for part in got:
        slot_grad = slot_grad + part.astype(F32)
    return token_grad, slot_grad[None], grad_gate, grad_up, grad_down


def solution(mesh):
    return jax.shard_map(
        functools.partial(per_device, mesh.shape["seq"], mesh.shape["grp"]),
        mesh=mesh,
        in_specs=(
            P("grp", "seq", None),
            P("grp", "seq", None),
            P("grp", "seq", None),
            P("grp", "seq", None),
            P("seq", None),
            P("seq", "grp", None),
            P("seq", "grp", None),
            P("seq", "grp", None),
        ),
        out_specs=(
            P("grp", "seq", None),
            P("grp", "seq", None),
            P("seq", "grp", None),
            P("seq", "grp", None),
            P("seq", "grp", None),
        ),
        check_vma=False,
    )
```

time: 37.8 us -> 32.4 us (0.86); the launches traced: 37.1 us -> 32.2 us
  Pallas kernels: 36.5 us -> 29.8 us
  starting transfers between devices: 0 us -> 1.09 us
  other arithmetic: 0 us -> 0.61 us
    pallas_call x1, Pallas kernels: 27.3 us -> 16.1 us  [per_device(): pl.pallas_call(functools.partial(exchange_kernel, nseq, ngrp), out_shape=...]
    pallas_call x1 -> x2, Pallas kernels: 9.2 us -> 13.7 us  [the longest x1 9.25 us: per_device(): pl.pallas_call(functools.partial(first_kernel, experts, cut), out_shape=(...]
    ppermute x0 -> x1, starting transfers between devices: none -> 1.09 us  [per_device(): lax.ppermute(sends[d - 1], 'grp', [(g, (g + d) % ngrp) for g in range(ngr...]
    broadcast_in_dim x0 -> x1, other arithmetic: none -> 0.61 us  [per_device(): return (token_grad, slot_grad[None], grad_gate, grad_up, grad_down)]
  transfers between devices with their start and end apart: 0 -> 1, of which waited for: 0 -> 0; matrix products, arithmetic and copies ran while one was open for 0% -> 0% of each run, Pallas kernels for 0% -> 14%
where the time goes in v1:
time: 32.4 us; the launch traced here: 32.2 us
  Pallas kernels  29.8 us (92%)
  starting transfers between devices  1.09 us (3%)
  between operations  0.67 us (2%)
  other arithmetic  0.61 us (2%)
    pallas_call x1, Pallas kernels, per_device(): pl.pallas_call(functools.partial(exchange_kernel, nseq, ngrp), out_shape=...  16.1 us
    pallas_call x1, Pallas kernels, per_device(): pl.pallas_call(functools.partial(first_kernel, experts, cut), out_shape=(...  9.25 us
    pallas_call x1, Pallas kernels, per_device(): pl.pallas_call(functools.partial(second_kernel, experts, cut), out_shape=...  4.47 us
    ppermute x1, starting transfers between devices, per_device(): lax.ppermute(sends[d - 1], 'grp', [(g, (g + d) % ngrp) for g in range(ngr...  1.09 us
  transfers between devices with their start and end apart: 1, of which 0 were waited for; matrix products, arithmetic and copies ran while one was open for 0% of the time, Pallas kernels for 14%

profile of v1, /device:TPU:0, one launch (start us, length us, event | category | flops | bytes accessed | tf_op | source)
XLA Modules:
  0.0 32.2 jit_solution(6262613426836194187)
XLA Ops:
  0.6 16.1 %exchange.1 = (bf16[4,1024,1024]{2,1,0:T(8,128)(2,1)S(1)}, bf16[4,1024,1024]{2,1,0:T(8,128)(2,1)S(1)}, bf16[4,1024,1024]{2,1,0:T(8,128)(2,1)S(1)}, bf16[216,1024...) custom-call(bf16[1,216,1024]{2,1,0:T(8,128)(2,1)} %grad_hbm.1, ...), custom_call_target="tpu_custom_call" | custom-call | tf_op jit(solution)/shard_map/exchange/pallas_call | solution.py:284
  16.8 9.2 %first.1 = (bf16[8,1024]{1,0:T(8,128)(2,1)S(1)}, f32[4,1024]{1,0:T(4,128)S(1)}, bf16[1,4,1024]{2,1,0:T(4,128)(2,1)S(1)}, bf16[4,1024,1024]{2,1,0:T(8,128)(2,1)}, bf16[4,1024,1024]{2,1,0:T(8,128)(2,1)}) custom-call(bf16[4,1024,1024]{2,1,0:T(8,128)(2,1)S(1)} %get-tuple-element.22.gate_w, bf16[4,1024,1024]{2,1,0:T(8,128)(2,1)S(1)} %get-tuple-element.23.up_w, ...), custom_call_target="tpu_custom_call" | custom-call | tf_op jit(solution)/shard_map/first/pallas_call | solution.py:315
  26.0 1.1 %collective-permute-start = (bf16[4,1024]{1,0:T(4,128)(2,1)S(1)}, bf16[4,1024]{1,0:T(4,128)(2,1)S(1)}, u32[]{:S(2)}, u32[]{:S(2)}) collective-permute-start(bf16[4,1024]{1,0:T(4,128)(2,1)S(1)} %bitcast.6), channel_id=1, source_target_pairs={{0,1},{1,0},{2,3},{3,2},{4,5},{5,4},{6,7},{7,6},{8,9},{9,8},{10,11... | collective-permute-start | bytes 24584 | tf_op jit(solution)/shard_map/ppermute | solution.py:334
  27.1 4.5 %second.1 = (bf16[1,216,1024]{2,1,0:T(8,128)(2,1)}, bf16[4,1024,1024]{2,1,0:T(8,128)(2,1)}) custom-call(bf16[8,1024]{1,0:T(8,128)(2,1)S(1)} %get-tuple-element.28.gg_ref, bf16[2,8,1024]{2,1,0:T(8,128)(2,1)S(1)} %get-tuple-element.27.pair_ref, f32[64,216]{1,0:T(8,128)S(1)} %get-tuple-element.29.probs_ref, bf16[216,1024]{1,0:T(8,128)(2,1)S(1)} %get-tuple-element.30.grad_ref, ...), custom_call_target="tpu_custom_call" | custom-call | bytes 8388608 | tf_op jit(solution)/shard_map/second/pallas_call | solution.py:338
  31.6 0.0 collective-permute-done
  31.6 0.6 %add_bitcast_fusion = f32[1,4,1024]{2,1,0:T(4,128)} fusion(f32[4,1024]{1,0:T(4,128)S(1)} %get-tuple-element.34, bf16[4,1024]{1,0:T(4,128)(2,1)S(1)} %collective-permute-done), kind=kLoop, calls=%fused_computation | loop fusion | flops 8192 | bytes 40960 | tf_op jit(solution)/shard_map/broadcast_in_dim | solution.py:357
Async XLA Ops:
  26.0 5.6 %collective-permute-start = (bf16[4,1024]{1,0:T(4,128)(2,1)S(1)}, bf16[4,1024]{1,0:T(4,128)(2,1)S(1)}, u32[]{:S(2)}, u32[]{:S(2)}) collective-permute-start(bf16[4,1024]{1,0:T(4,128)(2,1)S(1)} %bitcast.6), channel_id=1, source_target_pairs={{0,1},{1,0},{2,3},{3,2},{4,5},{5,4},{6,7},{7,6},{8,9},{9,8},{10,11... | collective-permute-start | bytes 24584 | tf_op jit(solution)/shard_map/ppermute | solution.py:334

commit v2 on v1

--- a/solution.py
+++ b/solution.py
@@ -168,19 +168,32 @@
     each(1, ngrp, lambda d: grp_copy(d, outs, out_ssem, out_rsem).wait_send())
 
 
-def mxu_outer(a, v, cut, store):
-    for j in range(a.shape[1] // cut):
-        at = slice(j * cut, (j + 1) * cut)
-        store(j, lax.dot_general(a[:, at], v, TN, preferred_element_type=F32).astype(BF16))
-
-
-def vpu_outer(a_cols, v_rows, cut, store):
-    for j in range(a_cols[0].shape[0] // cut):
-        at = slice(j * cut, (j + 1) * cut)
-        total = a_cols[0][at] * v_rows[0]
-        for a, v in zip(a_cols[1:], v_rows[1:]):
-            total += a[at] * v
-        store(j, total.astype(BF16))
+def mxu_outer(a, v, dst):
+    dst[...] = lax.dot_general(a, v, TN, preferred_element_type=F32).astype(BF16)
+
+
+def picker(experts, e, rows, lanes=128):
+    row = lax.broadcasted_iota(jnp.int32, (rows, lanes * (rows // experts)), 0)
+    lane = lax.broadcasted_iota(jnp.int32, (rows, lanes * (rows // experts)), 1)
+    return jnp.where(row == (lane // lanes) * experts + e, 1.0, 0.0).astype(BF16)
+
+
+def vpu_outer(experts, e, a, v, dst, lanes=128, step=16):
+    rows, dim = v.shape
+    spread = lax.dot_general(a, picker(experts, e, rows, lanes), TN, preferred_element_type=F32).astype(BF16)
+    tiles = [
+        [jnp.broadcast_to(v[r:r + 1, l:l + lanes], (step, lanes)) for l in range(0, dim, lanes)]
+        for r in range(e, rows, experts)
+    ]
+    for i in range(0, a.shape[1], step):
+        out = []
+        for l in range(dim // lanes):
+            total = None
+            for g, row in enumerate(tiles):
+                term = spread[i:i + step, g * lanes:(g + 1) * lanes] * row[l]
+                total = term if total is None else total + term
+            out.append(total)
+        dst[i:i + step] = jnp.concatenate(out, axis=1)
 
 
 def first_kernel(
@@ -192,33 +205,42 @@
     outs = (gd_hbm, gu_hbm)
     rows, width = hid_ref.shape
     ngrp = rows // experts
-    own = lax.rem(lax.broadcasted_iota(jnp.int32, (rows, width), 0), experts)
+    own = lax.rem(lax.broadcasted_iota(jnp.int32, (rows, cut), 0), experts)
+    x, so = pair_ref[0], pair_ref[1]
 
     def chunk(k, e, j):
         at = pl.ds(j * cut, cut)
         return pltpu.make_async_copy(staged.at[k, e, at], outs[k].at[e, at], sem.at[k, e, j])
 
-    def put(k, e):
-        def store(j, value):
-            staged[k, e, j * cut:(j + 1) * cut] = value
-            chunk(k, e, j).start()
-        return store
-
-    x, so = pair_ref[0], pair_ref[1]
-    hid = hid_ref[...].astype(F32)
+    def put(k, e, j, a, v):
+        vpu_outer(experts, e, a, v, staged.at[k, e, pl.ds(j * cut, cut)])
+        chunk(k, e, j).start()
+
+    def spread(e, j, gate_grad, up_grad, total):
+        at = slice(j * cut, (j + 1) * cut)
+        total += jnp.dot(gate_grad, gate_w[e, at], preferred_element_type=F32)
+        total += jnp.dot(up_grad, up_w[e, at], preferred_element_type=F32)
+        put(1, e, j, up_grad, x)
+        return total
+
     total = jnp.zeros((rows, x.shape[1]), F32)
-    gate_all = jnp.zeros((rows, width), F32)
-    for e in range(experts):
-        mine = own == e
-        mxu_outer(jnp.where(mine, hid, 0.0).astype(BF16), so, cut, put(0, e))
-        hgrad = lax.dot_general(so, down_w[e], NT, preferred_element_type=F32)
-        up_grad = jnp.where(mine, hgrad * acts_ref[1], 0.0).astype(BF16)
-        gate_f = jnp.where(mine, hgrad * acts_ref[0], 0.0)
-        gate_all += gate_f
-        mxu_outer(up_grad, x, cut, put(1, e))
-        total += jnp.dot(gate_f.astype(BF16), gate_w[e], preferred_element_type=F32)
-        total += jnp.dot(up_grad, up_w[e], preferred_element_type=F32)
-    gg_ref[...] = gate_all.astype(BF16)
+    gate_all = [jnp.zeros((rows, cut), F32)] * (width // cut)
+    late = []
+    for e in range(experts):
+        for j in range(width // cut):
+            at = slice(j * cut, (j + 1) * cut)
+            hgrad = lax.dot_general(so, down_w[e, at], NT, preferred_element_type=F32)
+            put(0, e, j, hid_ref[:, at], so)
+            gate_f = jnp.where(own == e, hgrad * acts_ref[0, :, at], 0.0)
+            gate_all[j] += gate_f
+            up_grad = jnp.where(own == e, hgrad * acts_ref[1, :, at], 0.0).astype(BF16)
+            late.append((e, j, gate_f.astype(BF16), up_grad))
+            if len(late) > 1:
+                total = spread(*late.pop(0), total)
+    for item in late:
+        total = spread(*item, total)
+    for j in range(width // cut):
+        gg_ref[:, j * cut:(j + 1) * cut] = gate_all[j].astype(BF16)
     g_me = lax.axis_index("grp")
     for d in range(ngrp):
         at = lax.rem(g_me + d, ngrp)
@@ -242,30 +264,26 @@
     staged, tokens, sem, small_sem,
 ):
     rows, width = gg_ref.shape
-    own = lax.rem(lax.broadcasted_iota(jnp.int32, (rows, width), 0), experts)
 
     def chunk(e, j):
         at = pl.ds(j * cut, cut)
         return pltpu.make_async_copy(staged.at[e, at], gg_hbm.at[e, at], sem.at[e, j])
 
-    def put(e):
-        def store(j, value):
-            staged[e, j * cut:(j + 1) * cut] = value
+    x = pair_ref[0]
+    small = None
+    for e in range(experts):
+        for j in range(width // cut):
+            at = slice(j * cut, (j + 1) * cut)
+            vpu_outer(experts, e, gg_ref[:, at], x, staged.at[e, at])
             chunk(e, j).start()
-        return store
-
-    x = pair_ref[0]
-    gate_grad = gg_ref[...].astype(F32)
-    for e in range(experts):
-        mxu_outer(jnp.where(own == e, gate_grad, 0.0).astype(BF16), x, cut, put(e))
-        if e == 0:
-            wgrad = lax.dot_general(eout_ref[...], grad_ref[...], NT, preferred_element_type=F32)
-            p = probs_ref[...]
-            centre = jnp.sum(wgrad * p, axis=0, keepdims=True)
-            lgrad = (p * (wgrad - centre)).astype(BF16)
-            tokens[...] = lax.dot_general(lgrad, rout_ref[...], TN, preferred_element_type=F32).astype(BF16)
-            small = pltpu.make_async_copy(tokens, tgrad_hbm.at[0], small_sem.at[0])
-            small.start()
+            if small is None:
+                wgrad = lax.dot_general(eout_ref[...], grad_ref[...], NT, preferred_element_type=F32)
+                p = probs_ref[...]
+                centre = jnp.sum(wgrad * p, axis=0, keepdims=True)
+                lgrad = (p * (wgrad - centre)).astype(BF16)
+                tokens[...] = lax.dot_general(lgrad, rout_ref[...], TN, preferred_element_type=F32).astype(BF16)
+                small = pltpu.make_async_copy(tokens, tgrad_hbm.at[0], small_sem.at[0])
+                small.start()
     for e in range(experts):
         for j in range(width // cut):
             chunk(e, j).wait()
@@ -326,7 +344,7 @@
             pltpu.VMEM((2, experts, width, dim), BF16),
             DMA((2, experts, width // cut)),
         ],
-        compiler_params=pltpu.CompilerParams(vmem_limit_bytes=20 * 1024 * 1024),
+        compiler_params=pltpu.CompilerParams(vmem_limit_bytes=26 * 1024 * 1024),
         name="first",
     )(gate_w, up_w, down_w, acts, hid, pair)
 
@@ -346,7 +364,7 @@
             DMA((experts, width // cut)),
             DMA((1,)),
         ],
-        compiler_params=pltpu.CompilerParams(vmem_limit_bytes=12 * 1024 * 1024),
+        compiler_params=pltpu.CompilerParams(vmem_limit_bytes=20 * 1024 * 1024),
         cost_estimate=pl.CostEstimate(
             flops=0, bytes_accessed=experts * width * dim * 2, transcendentals=0),
         name="second",

time: 32.4 us -> 29.7 us (0.917)
  Pallas kernels: 29.8 us -> 27.1 us
    pallas_call x1, Pallas kernels: 9.25 us -> 7.01 us  [per_device(): pl.pallas_call(functools.partial(first_kernel, experts, cut), out_shape=(...]
where the time goes in v2:
time: 29.7 us; the launch traced here: 29.5 us
  Pallas kernels  27.1 us (91%)
  starting transfers between devices  1.09 us (4%)
  between operations  0.67 us (2%)
  other arithmetic  0.61 us (2%)
    pallas_call x1, Pallas kernels, per_device(): pl.pallas_call(functools.partial(exchange_kernel, nseq, ngrp), out_shape=...  15.9 us
    pallas_call x1, Pallas kernels, per_device(): pl.pallas_call(functools.partial(first_kernel, experts, cut), out_shape=(...  7.01 us
    pallas_call x1, Pallas kernels, per_device(): pl.pallas_call(functools.partial(second_kernel, experts, cut), out_shape=...  4.19 us
    ppermute x1, starting transfers between devices, per_device(): lax.ppermute(sends[d - 1], 'grp', [(g, (g + d) % ngrp) for g in range(ngr...  1.09 us
    broadcast_in_dim x1, other arithmetic, per_device(): return (token_grad, slot_grad[None], grad_gate, grad_up, grad_down)  0.61 us
  transfers between devices with their start and end apart: 1, of which 0 were waited for; matrix products, arithmetic and copies ran while one was open for 0% of the time, Pallas kernels for 14%

profile of v2, /device:TPU:0, one launch (start us, length us, event | category | flops | bytes accessed | tf_op | source)
XLA Modules:
  0.0 29.5 jit_solution(17155483795303396595)
XLA Ops:
  0.6 15.9 %exchange.1 = (bf16[4,1024,1024]{2,1,0:T(8,128)(2,1)S(1)}, bf16[4,1024,1024]{2,1,0:T(8,128)(2,1)S(1)}, bf16[4,1024,1024]{2,1,0:T(8,128)(2,1)S(1)}, bf16[216,1024...) custom-call(bf16[1,216,1024]{2,1,0:T(8,128)(2,1)} %grad_hbm.1, ...), custom_call_target="tpu_custom_call" | custom-call | tf_op jit(solution)/shard_map/exchange/pallas_call | solution.py:302
  16.6 7.0 %first.1 = (bf16[8,1024]{1,0:T(8,128)(2,1)S(1)}, f32[4,1024]{1,0:T(4,128)S(1)}, bf16[1,4,1024]{2,1,0:T(4,128)(2,1)S(1)}, bf16[4,1024,1024]{2,1,0:T(8,128)(2,1)}, bf16[4,1024,1024]{2,1,0:T(8,128)(2,1)}) custom-call(bf16[4,1024,1024]{2,1,0:T(8,128)(2,1)S(1)} %get-tuple-element.22.gate_w, bf16[4,1024,1024]{2,1,0:T(8,128)(2,1)S(1)} %get-tuple-element.23.up_w, ...), custom_call_target="tpu_custom_call" | custom-call | tf_op jit(solution)/shard_map/first/pallas_call | solution.py:333
  23.6 1.1 %collective-permute-start = (bf16[4,1024]{1,0:T(4,128)(2,1)S(1)}, bf16[4,1024]{1,0:T(4,128)(2,1)S(1)}, u32[]{:S(2)}, u32[]{:S(2)}) collective-permute-start(bf16[4,1024]{1,0:T(4,128)(2,1)S(1)} %bitcast.6), channel_id=1, source_target_pairs={{0,1},{1,0},{2,3},{3,2},{4,5},{5,4},{6,7},{7,6},{8,9},{9,8},{10,11... | collective-permute-start | bytes 24584 | tf_op jit(solution)/shard_map/ppermute | solution.py:352
  24.7 4.2 %second.1 = (bf16[1,216,1024]{2,1,0:T(8,128)(2,1)}, bf16[4,1024,1024]{2,1,0:T(8,128)(2,1)}) custom-call(bf16[8,1024]{1,0:T(8,128)(2,1)S(1)} %get-tuple-element.28.gg_ref, bf16[2,8,1024]{2,1,0:T(8,128)(2,1)S(1)} %get-tuple-element.27.pair_ref, f32[64,216]{1,0:T(8,128)S(1)} %get-tuple-element.29.probs_ref, bf16[216,1024]{1,0:T(8,128)(2,1)S(1)} %get-tuple-element.30.grad_ref, ...), custom_call_target="tpu_custom_call" | custom-call | bytes 8388608 | tf_op jit(solution)/shard_map/second/pallas_call | solution.py:356
  28.9 0.0 collective-permute-done
  28.9 0.6 %add_bitcast_fusion = f32[1,4,1024]{2,1,0:T(4,128)} fusion(f32[4,1024]{1,0:T(4,128)S(1)} %get-tuple-element.34, bf16[4,1024]{1,0:T(4,128)(2,1)S(1)} %collective-permute-done), kind=kLoop, calls=%fused_computation | loop fusion | flops 8192 | bytes 40960 | tf_op jit(solution)/shard_map/broadcast_in_dim | solution.py:375
Async XLA Ops:
  23.6 5.3 %collective-permute-start = (bf16[4,1024]{1,0:T(4,128)(2,1)S(1)}, bf16[4,1024]{1,0:T(4,128)(2,1)S(1)}, u32[]{:S(2)}, u32[]{:S(2)}) collective-permute-start(bf16[4,1024]{1,0:T(4,128)(2,1)S(1)} %bitcast.6), channel_id=1, source_target_pairs={{0,1},{1,0},{2,3},{3,2},{4,5},{5,4},{6,7},{7,6},{8,9},{9,8},{10,11... | collective-permute-start | bytes 24584 | tf_op jit(solution)/shard_map/ppermute | solution.py:352

commit v3 on v2

--- a/solution.py
+++ b/solution.py
@@ -40,9 +40,6 @@
         pl.semaphore_signal(barrier, inc=1, device_id={"grp": lax.rem(g_me + d, ngrp)}, device_id_type=MESH)
         return c
 
-    lax.fori_loop(1, ngrp, greet_grp, 0)
-    lax.fori_loop(1, nseq, greet_seq, 0)
-
     loads = [
         pltpu.make_async_copy(logit_hbm, probs_ref, load_sem.at[0]),
         pltpu.make_async_copy(grad_hbm.at[0], grad, load_sem.at[1]),
@@ -52,6 +49,9 @@
     ]
     for c in loads:
         c.start()
+
+    lax.fori_loop(1, ngrp, greet_grp, 0)
+    lax.fori_loop(1, nseq, greet_seq, 0)
     w_loads = {}
     for m, (src, dst) in enumerate(((gate_hbm, gate_w), (up_hbm, up_w), (down_hbm, down_w))):
         for e in range(experts):
@@ -115,8 +115,8 @@
         c.wait()
 
     pl.semaphore_wait(barrier, (nseq - 1) + (ngrp - 1))
+    each(1, nseq, lambda d: part_copy(d).start())
     each(1, ngrp, lambda d: grp_copy(d, slots, slot_ssem, slot_rsem).start())
-    each(1, nseq, lambda d: part_copy(d).start())
     each(1, nseq, lambda d: piece_copy(d).start())
 
     rows = ngrp * experts
@@ -226,17 +226,26 @@
     total = jnp.zeros((rows, x.shape[1]), F32)
     gate_all = [jnp.zeros((rows, cut), F32)] * (width // cut)
     late = []
-    for e in range(experts):
-        for j in range(width // cut):
-            at = slice(j * cut, (j + 1) * cut)
-            hgrad = lax.dot_general(so, down_w[e, at], NT, preferred_element_type=F32)
-            put(0, e, j, hid_ref[:, at], so)
-            gate_f = jnp.where(own == e, hgrad * acts_ref[0, :, at], 0.0)
-            gate_all[j] += gate_f
-            up_grad = jnp.where(own == e, hgrad * acts_ref[1, :, at], 0.0).astype(BF16)
-            late.append((e, j, gate_f.astype(BF16), up_grad))
-            if len(late) > 1:
-                total = spread(*late.pop(0), total)
+    spots = [(e, j) for e in range(experts) for j in range(width // cut)]
+    lead = 1
+
+    def down(t):
+        e, j = spots[t]
+        put(0, e, j, hid_ref[:, j * cut:(j + 1) * cut], so)
+
+    for t in range(lead):
+        down(t)
+    for t, (e, j) in enumerate(spots):
+        at = slice(j * cut, (j + 1) * cut)
+        hgrad = lax.dot_general(so, down_w[e, at], NT, preferred_element_type=F32)
+        if t + lead < len(spots):
+            down(t + lead)
+        gate_f = jnp.where(own == e, hgrad * acts_ref[0, :, at], 0.0)
+        gate_all[j] += gate_f
+        up_grad = jnp.where(own == e, hgrad * acts_ref[1, :, at], 0.0).astype(BF16)
+        late.append((e, j, gate_f.astype(BF16), up_grad))
+        if len(late) > 1:
+            total = spread(*late.pop(0), total)
     for item in late:
         total = spread(*item, total)
     for j in range(width // cut):
@@ -270,13 +279,12 @@
         return pltpu.make_async_copy(staged.at[e, at], gg_hbm.at[e, at], sem.at[e, j])
 
     x = pair_ref[0]
-    small = None
     for e in range(experts):
         for j in range(width // cut):
             at = slice(j * cut, (j + 1) * cut)
             vpu_outer(experts, e, gg_ref[:, at], x, staged.at[e, at])
             chunk(e, j).start()
-            if small is None:
+            if e * (width // cut) + j == min(11, experts * (width // cut) - 1):
                 wgrad = lax.dot_general(eout_ref[...], grad_ref[...], NT, preferred_element_type=F32)
                 p = probs_ref[...]
                 centre = jnp.sum(wgrad * p, axis=0, keepdims=True)

time: 29.7 us -> 29.1 us (0.980)
  Pallas kernels: 27.1 us -> 26.6 us
    pallas_call x1, Pallas kernels: 4.19 us -> 3.83 us  [per_device(): pl.pallas_call(functools.partial(second_kernel, experts, cut), out_shape=...]
  transfers between devices with their start and end apart: 1 -> 1, of which waited for: 0 -> 0; matrix products, arithmetic and copies ran while one was open for 0% -> 0% of each run, Pallas kernels for 14% -> 13%
where the time goes in v3:
time: 29.1 us; the launch traced here: 28.9 us
  Pallas kernels  26.6 us (91%)
  starting transfers between devices  1.04 us (4%)
  between operations  0.67 us (2%)
  other arithmetic  0.61 us (2%)
    pallas_call x1, Pallas kernels, per_device(): pl.pallas_call(functools.partial(exchange_kernel, nseq, ngrp), out_shape=...  15.9 us
    pallas_call x1, Pallas kernels, per_device(): pl.pallas_call(functools.partial(first_kernel, experts, cut), out_shape=(...  6.84 us
    pallas_call x1, Pallas kernels, per_device(): pl.pallas_call(functools.partial(second_kernel, experts, cut), out_shape=...  3.83 us
    ppermute x1, starting transfers between devices, per_device(): lax.ppermute(sends[d - 1], 'grp', [(g, (g + d) % ngrp) for g in range(ngr...  1.04 us
    broadcast_in_dim x1, other arithmetic, per_device(): return (token_grad, slot_grad[None], grad_gate, grad_up, grad_down)  0.61 us
  transfers between devices with their start and end apart: 1, of which 0 were waited for; matrix products, arithmetic and copies ran while one was open for 0% of the time, Pallas kernels for 13%

profile of v3, /device:TPU:0, one launch (start us, length us, event | category | flops | bytes accessed | tf_op | source)
XLA Modules:
  0.0 28.9 jit_solution(17937637538646598820)
XLA Ops:
  0.6 15.9 %exchange.1 = (bf16[4,1024,1024]{2,1,0:T(8,128)(2,1)S(1)}, bf16[4,1024,1024]{2,1,0:T(8,128)(2,1)S(1)}, bf16[4,1024,1024]{2,1,0:T(8,128)(2,1)S(1)}, bf16[216,1024...) custom-call(bf16[1,216,1024]{2,1,0:T(8,128)(2,1)} %grad_hbm.1, ...), custom_call_target="tpu_custom_call" | custom-call | tf_op jit(solution)/shard_map/exchange/pallas_call | solution.py:310
  16.6 6.8 %first.1 = (bf16[8,1024]{1,0:T(8,128)(2,1)S(1)}, f32[4,1024]{1,0:T(4,128)S(1)}, bf16[1,4,1024]{2,1,0:T(4,128)(2,1)S(1)}, bf16[4,1024,1024]{2,1,0:T(8,128)(2,1)}, bf16[4,1024,1024]{2,1,0:T(8,128)(2,1)}) custom-call(bf16[4,1024,1024]{2,1,0:T(8,128)(2,1)S(1)} %get-tuple-element.22.gate_w, bf16[4,1024,1024]{2,1,0:T(8,128)(2,1)S(1)} %get-tuple-element.23.up_w, ...), custom_call_target="tpu_custom_call" | custom-call | tf_op jit(solution)/shard_map/first/pallas_call | solution.py:341
  23.4 1.0 %collective-permute-start = (bf16[4,1024]{1,0:T(4,128)(2,1)S(1)}, bf16[4,1024]{1,0:T(4,128)(2,1)S(1)}, u32[]{:S(2)}, u32[]{:S(2)}) collective-permute-start(bf16[4,1024]{1,0:T(4,128)(2,1)S(1)} %bitcast.6), channel_id=1, source_target_pairs={{0,1},{1,0},{2,3},{3,2},{4,5},{5,4},{6,7},{7,6},{8,9},{9,8},{10,11... | collective-permute-start | bytes 24584 | tf_op jit(solution)/shard_map/ppermute | solution.py:360
  24.5 3.8 %second.1 = (bf16[1,216,1024]{2,1,0:T(8,128)(2,1)}, bf16[4,1024,1024]{2,1,0:T(8,128)(2,1)}) custom-call(bf16[8,1024]{1,0:T(8,128)(2,1)S(1)} %get-tuple-element.28.gg_ref, bf16[2,8,1024]{2,1,0:T(8,128)(2,1)S(1)} %get-tuple-element.27.pair_ref, f32[64,216]{1,0:T(8,128)S(1)} %get-tuple-element.29.probs_ref, bf16[216,1024]{1,0:T(8,128)(2,1)S(1)} %get-tuple-element.30.grad_ref, ...), custom_call_target="tpu_custom_call" | custom-call | bytes 8388608 | tf_op jit(solution)/shard_map/second/pallas_call | solution.py:364
  28.3 0.0 collective-permute-done
  28.3 0.6 %add_bitcast_fusion = f32[1,4,1024]{2,1,0:T(4,128)} fusion(f32[4,1024]{1,0:T(4,128)S(1)} %get-tuple-element.34, bf16[4,1024]{1,0:T(4,128)(2,1)S(1)} %collective-permute-done), kind=kLoop, calls=%fused_computation | loop fusion | flops 8192 | bytes 40960 | tf_op jit(solution)/shard_map/broadcast_in_dim | solution.py:383
Async XLA Ops:
  23.4 4.9 %collective-permute-start = (bf16[4,1024]{1,0:T(4,128)(2,1)S(1)}, bf16[4,1024]{1,0:T(4,128)(2,1)S(1)}, u32[]{:S(2)}, u32[]{:S(2)}) collective-permute-start(bf16[4,1024]{1,0:T(4,128)(2,1)S(1)} %bitcast.6), channel_id=1, source_target_pairs={{0,1},{1,0},{2,3},{3,2},{4,5},{5,4},{6,7},{7,6},{8,9},{9,8},{10,11... | collective-permute-start | bytes 24584 | tf_op jit(solution)/shard_map/ppermute | solution.py:360
